TPU v7x, 256 devices: a whole 4x4x8 slice. The times are simulated.
256 devices in a mesh: row: 8 (over x, y_hi), col: 32 (over z, y_lo, core).
Axes of the slice: x: 4, y: 4 (y_hi: 2, y_lo: 2; y = y_hi * 2 + y_lo), z: 8, core: 2. Of those that a mesh axis runs over, the one named last changes fastest.
Arguments:
- grams: bfloat16 [4, 8, 32, 32, 8192], P(None, None, 'col', None, 'row'), may hold values from -2.6 to 32, as said below
- adjusted: bfloat16 [4, 8192, 1024], P(None, ('row', 'col')), may hold values from -6 to 6
Outputs:
- merged: float32 [8192, 1024], P(('row', 'col'))
- residual_norms: float32 [3], replicated
Inputs may be any that keep to these rules, and one draw needn't show every extreme that they name: `grams`: each G_m is symmetric positive definite.
All inputs are finite; a program needn't handle non-finite values.
Results may differ from a plain program's by a relative error of at most 0.0041.
Values may be sent and summed in bfloat16 or wider, within the bound.
A program may use at most 64 MiB of HBM per device.

v0:
```python
import jax
import jax.numpy as jnp
from jax import lax
from jax.sharding import Mesh
from jax.sharding import PartitionSpec as P

SWEEPS = 3
COL = ("col_0", "col_1", "col_2")
ROW = ("row_0", "row_1")
ROW_COL = ("row_0", "row_1", "col_0", "col_1", "col_2")
SHRINK = 0.9


def split_up(value, dim, peers):
    dims = value.shape
    tiles = value.reshape(*dims[:dim], peers, dims[dim] // peers, *dims[dim + 1 :])
    return jnp.moveaxis(tiles, dim, 0)


def sum_at_owner(value, axis, dim):
    tiles = split_up(value, dim, lax.axis_size(axis))
    arrived = lax.all_to_all(tiles, axis, split_axis=0, concat_axis=0, tiled=True)
    return arrived.sum(axis=0)


def one_axis_at_a_time(value, axes):
    for axis in axes:
        value = lax.psum(value, axis)
    return value


def block_solve(factor, rows):
    lower = lax.linalg.triangular_solve(factor, rows, left_side=True, lower=True)
    return lax.linalg.triangular_solve(factor, lower, left_side=True, lower=True, transpose_a=True)


def apply_gram(gram_flat, operand):
    panels = lax.all_gather(operand, COL, axis=1, tiled=True)
    partial_value = lax.slice_in_dim(gram_flat, 0, operand.shape[1] * lax.axis_size(ROW), axis=1)
    return sum_at_owner(
        jnp.einsum("ksi,kio->so", partial_value, panels, preferred_element_type=jnp.float32), ROW, 0
    )


def local(grams, adjusted):
    models = grams.shape[0]
    major = grams.shape[1]
    sub_rows = grams.shape[3]
    columns = grams.shape[4]
    here_row = lax.axis_index(ROW)
    here_col = lax.axis_index(COL)
    gram_flat = grams.reshape(models, major * sub_rows, columns)
    total32 = jnp.sum(grams.astype(jnp.float32), axis=0)
    gram_total = total32.astype(jnp.bfloat16).reshape(1, major * sub_rows, columns)
    own_rows = lax.dynamic_slice_in_dim(grams[:, :, 0], here_row, 1, 1)[:, 0]
    own_block = lax.dynamic_slice_in_dim(own_rows, here_col * sub_rows, sub_rows, 2).astype(
        jnp.float32
    )
    diag_each = jnp.diagonal(own_block, axis1=1, axis2=2)
    diag_sum = jnp.sum(diag_each, 0)
    precond = SHRINK * jnp.sum(own_block, 0) + (1.0 - SHRINK) * jnp.diag(diag_sum)
    factor = jnp.linalg.cholesky(precond)
    weights32 = adjusted.astype(jnp.float32)
    rhs = SHRINK * apply_gram(gram_flat, adjusted)
    rhs = rhs + (1.0 - SHRINK) * jnp.sum(diag_each[:, :, None] * weights32, 0)
    rhs_local = jnp.sum(rhs * rhs)
    merged = jnp.mean(weights32, 0)
    squares_list = []
    for sweep_index in range(SWEEPS):
        image = SHRINK * apply_gram(gram_total, merged.astype(jnp.bfloat16)[None])
        image = image + (1.0 - SHRINK) * diag_sum[:, None] * merged
        resid = rhs - image
        squares_local = jnp.sum(resid * resid)
        squares_list.append(squares_local)
        merged = merged + block_solve(factor, resid)
    totals = one_axis_at_a_time(jnp.stack(squares_list + [rhs_local]), ROW_COL)
    norms = jnp.sqrt(totals[:SWEEPS] / totals[SWEEPS])
    return (merged, norms)


def solution(mesh):
    finer = Mesh(mesh.devices.reshape(4, 2, 8, 2, 2), ("row_0", "row_1", "col_0", "col_1", "col_2"))
    placed = (P(None, None, COL, None, ROW), P(None, ROW_COL, None))
    return jax.shard_map(
        local, mesh=finer, in_specs=placed, out_specs=(P(ROW_COL, None), P()), check_vma=False
    )
```

profile of v0, /device:TPU:1, one launch (start us, length us, event | category | flops | bytes accessed | tf_op | source)
XLA Modules:
  0.0 421.2 jit_solution(12293854520328392393)
XLA Ops:
  7.3 1.5 copy-done
  8.8 0.1 constant_dynamic-slice_fusion
  8.9 0.3 copy.16
  9.2 0.7 gather_fusion
  10.0 1.1 convert_reduce_fusion.1
  11.1 0.6 multiply_convert_fusion
  11.8 0.7 all-gather.8.cloned.1.call-update
  12.5 0.4 reduce_sum.125
  13.0 67.6 %all-gather.10.cloned.1.call-done = bf16[1024,1024]{1,0:T(8,128)(2,1)} async-done(((bf16[32,1024]{1,0:T(8,128)(2,1)}), bf16[1024,1024]{1,0:T(8,128)(2,1)}) %all-gather.10.cloned.1.call-update) | async-done | bytes 2097168 | tf_op jit(solution)/shard_map/all_gather | solution.py:38
  80.5 3.3 fusion.7
  83.8 6.1 %all-to-all-start.1 = ((f32[8,32,1024]{2,1,0:T(8,128)}), f32[8,32,1024]{2,1,0:T(8,128)}, u32[]{:S(2)}, u32[]{:S(2)}) async-start(f32[8,32,1024]{2,1,0:T(8,128)} %fusion.7), calls=%async_computation.1 | async-start | bytes 2097152 | tf_op jit(solution)/shard_map/all_to_all | solution.py:22
  89.9 0.2 convert_reduce_fusion
  90.2 67.5 %all-gather.8.cloned.1.call-done = bf16[4,1024,1024]{2,1,0:T(8,128)(2,1)} async-done(((bf16[4,32,1024]{2,1,0:T(8,128)(2,1)}), bf16[4,1024,1024]{2,1,0:T(8,128)(2,1)}) %all-gather.8.cloned.1.call-update) | async-done | bytes 8388624 | tf_op jit(solution)/shard_map/all_gather | solution.py:38
  157.7 6.7 %fusion.9 = f32[8,32,1024]{2,1,0:T(8,128)} fusion(bf16[4,1024,1024]{2,1,0:T(8,128)(2,1)} %all-gather.8.cloned.1.call-done, bf16[4,8,1,32,1024]{4,3,2,1,0:T(8,128)(2,1)S(1)} %copy-done), kind=kOutput, calls=%fused_computation.10 | convolution fusion | flops 2147483648 | bytes 11534336 | tf_op jit(solution)/shard_map/ksi,kio->so/dot_general | solution.py:41
  164.4 7.1 %all-to-all-start = ((f32[8,32,1024]{2,1,0:T(8,128)}), f32[8,32,1024]{2,1,0:T(8,128)}, u32[]{:S(2)}, u32[]{:S(2)}) async-start(f32[8,32,1024]{2,1,0:T(8,128)} %fusion.9), calls=%async_computation | async-start | bytes 2097152 | tf_op jit(solution)/shard_map/all_to_all | solution.py:22
  171.6 0.1 reduce_sum.122
  171.8 0.1 fusion.26
  171.8 2.9 cholesky.19
  174.8 0.6 compare_reduce_fusion
  175.4 0.7 fusion.15
  176.1 2.4 custom-call.16
  178.5 1.3 reduce_sum.126
  179.9 7.6 %all-to-all-done = f32[8,32,1024]{2,1,0:T(8,128)} async-done(((f32[8,32,1024]{2,1,0:T(8,128)}), f32[8,32,1024]{2,1,0:T(8,128)}, u32[]{:S(2)}, u32[]{:S(2)}) %all-to-all-start) | async-done | bytes 1048608 | tf_op jit(solution)/shard_map/all_to_all | solution.py:22
  187.5 1.3 reduce_sum.123
  188.8 0.7 multiply_reduce_fusion.3
  189.5 0.3 fusion.22
  189.8 0.9 fusion.27
  190.8 62.2 %all-gather.12.cloned.1.call-done = bf16[1024,1024]{1,0:T(8,128)(2,1)} async-done(((bf16[32,1024]{1,0:T(8,128)(2,1)}), bf16[1024,1024]{1,0:T(8,128)(2,1)}) %all-gather.12.cloned.1.call-update) | async-done | bytes 2097168 | tf_op jit(solution)/shard_map/all_gather | solution.py:38
  253.0 2.3 fusion.5
  255.3 21.7 %all_to_all.20 = f32[8,32,1024]{2,1,0:T(8,128)} all-to-all(f32[8,32,1024]{2,1,0:T(8,128)S(1)} %fusion.5), channel_id=1, replica_groups=mesh['row_0'=4,'row_1'=2,'col_0'=8,'col_1'=2,'col_2'=2] {'row_0','row_1'}, dimensions={0} | all-to-all | bytes 2097152 | tf_op jit(solution)/shard_map/all_to_all | solution.py:22
  277.0 1.3 reduce_sum.127
  278.3 0.7 multiply_reduce_fusion.2
  279.0 0.3 fusion.19
  279.3 0.9 fusion.28
  280.2 62.7 %all-gather.14.cloned.1.call-done = bf16[1024,1024]{1,0:T(8,128)(2,1)} async-done(((bf16[32,1024]{1,0:T(8,128)(2,1)}), bf16[1024,1024]{1,0:T(8,128)(2,1)}) %all-gather.14.cloned.1.call-update) | async-done | bytes 2097168 | tf_op jit(solution)/shard_map/all_gather | solution.py:38
  342.9 2.3 fusion.3
  345.2 21.6 %all_to_all.21 = f32[8,32,1024]{2,1,0:T(8,128)S(1)} all-to-all(f32[8,32,1024]{2,1,0:T(8,128)S(1)} %fusion.3), channel_id=1, replica_groups=mesh['row_0'=4,'row_1'=2,'col_0'=8,'col_1'=2,'col_2'=2] {'row_0','row_1'}, dimensions={0} | all-to-all | bytes 2097152 | tf_op jit(solution)/shard_map/all_to_all | solution.py:22
  366.9 1.4 multiply_reduce_fusion.1
  368.3 2.7 pad_maximum_fusion
  371.0 6.9 %psum.35 = f32[4]{0:T(128)S(1)} all-reduce(f32[4]{0:T(128)S(1)} %pad_maximum_fusion), channel_id=1, replica_groups=mesh['row_0'=4,'row_1'=2,'col_0'=8,'col_1'=2,'col_2'=2] {'row_0'}, use_global_device_ids=true, to_apply=%region_15.18 | all-reduce | flops 4 | bytes 32 | tf_op jit(solution)/shard_map/psum | solution.py:28
  377.9 5.3 %psum.36 = f32[4]{0:T(128)S(1)} all-reduce(f32[4]{0:T(128)S(1)} %psum.35), channel_id=1, replica_groups=mesh['row_0'=4,'row_1'=2,'col_0'=8,'col_1'=2,'col_2'=2] {'row_1'}, use_global_device_ids=true, to_apply=%region_16.19 | all-reduce | flops 4 | bytes 32 | tf_op jit(solution)/shard_map/psum | solution.py:28
  383.1 12.5 %psum.37 = f32[4]{0:T(128)S(1)} all-reduce(f32[4]{0:T(128)S(1)} %psum.36), channel_id=1, replica_groups=mesh['row_0'=4,'row_1'=2,'col_0'=8,'col_1'=2,'col_2'=2] {'col_0'}, use_global_device_ids=true, to_apply=%region_17.20 | all-reduce | flops 4 | bytes 32 | tf_op jit(solution)/shard_map/psum | solution.py:28
  395.7 0.3 fusion.16
  396.0 4.1 psum.38
  400.1 0.9 convolution_add_fusion
  401.0 11.8 %psum.39 = f32[4]{0:T(128)S(1)} all-reduce(f32[4]{0:T(128)S(1)} %psum.38), channel_id=1, replica_groups=mesh['row_0'=4,'row_1'=2,'col_0'=8,'col_1'=2,'col_2'=2] {'col_2'}, use_global_device_ids=true, to_apply=%region_19.22 | all-reduce | flops 4 | bytes 32 | tf_op jit(solution)/shard_map/psum | solution.py:28
  412.8 0.7 slice.17
  413.4 1.2 divide_sqrt_fusion
  (20 shorter events, 0.6 us)
Async XLA Ops:
  7.2 1.6 copy-start
  7.2 73.4 %all-gather.10.cloned.1.call-start = ((), (), s32[]{:S(2)}) async-start(), calls=%async_computation.5 | async-start | bytes 2162688 | tf_op jit(solution)/shard_map/all_gather | solution.py:38
  11.8 146.0 %all-gather.8.cloned.1.call-start = ((), (), s32[]{:S(2)}) async-start(), calls=%async_computation.4 | async-start | bytes 8650752 | tf_op jit(solution)/shard_map/all_gather | solution.py:38
  83.8 80.6 %all-to-all-start.1 = ((f32[8,32,1024]{2,1,0:T(8,128)}), f32[8,32,1024]{2,1,0:T(8,128)}, u32[]{:S(2)}, u32[]{:S(2)}) async-start(f32[8,32,1024]{2,1,0:T(8,128)} %fusion.7), calls=%async_computation.1 | async-start | bytes 2097152 | tf_op jit(solution)/shard_map/all_to_all | solution.py:22
  164.4 23.0 %all-to-all-start = ((f32[8,32,1024]{2,1,0:T(8,128)}), f32[8,32,1024]{2,1,0:T(8,128)}, u32[]{:S(2)}, u32[]{:S(2)}) async-start(f32[8,32,1024]{2,1,0:T(8,128)} %fusion.9), calls=%async_computation | async-start | bytes 2097152 | tf_op jit(solution)/shard_map/all_to_all | solution.py:22
  171.5 81.4 %all-gather.12.cloned.1.call-start = ((), (), s32[]{:S(2)}) async-start(), calls=%async_computation.6 | async-start | bytes 2162688 | tf_op jit(solution)/shard_map/all_gather | solution.py:38
  178.5 99.7 %copy-start.1 = (f32[32]{0:T(128)}, f32[32]{0:T(128)S(1)}, u32[]{:S(2)}) copy-start(f32[32]{0:T(128)S(1)} %get-tuple-element.14) | copy-start | bytes 388
  190.7 152.2 %all-gather.14.cloned.1.call-start = ((), (), s32[]{:S(2)}) async-start(), calls=%async_computation.7 | async-start | bytes 2162688 | tf_op jit(solution)/shard_map/all_gather | solution.py:38
Sparse Core Ops, SparseCore 0:
  11.9 68.5 all-gather.9
  82.4 75.3 all-gather.7
  190.8 62.0 all-gather.11
  280.4 62.5 all-gather.13
where the time goes:
time: 422 us; the launch traced here: 421 us
  waiting for transfers between devices  268 us (64%)
  blocking collectives  83.9 us (20%)
  other arithmetic  20 us (5%)
  matrix products  18.2 us (4%)
  between operations  13.9 us (3%)
  starting transfers between devices  13.4 us (3%)
    all_gather x4, waiting for transfers between devices, apply_gram(): panels = lax.all_gather(operand, COL, axis=1, tiled=True)  260 us
    all_to_all x2, blocking collectives, sum_at_owner(): lax.all_to_all(tiles, axis, split_axis=0, concat_axis=0, tiled=True)  43.3 us
    psum x5, blocking collectives, one_axis_at_a_time(): value = lax.psum(value, axis)  40.5 us
    dot_general x4, matrix products, apply_gram(): jnp.einsum('ksi,kio->so', partial_value, panels, preferred_element_type=j...  14.5 us
    all_to_all x2, starting transfers between devices, sum_at_owner(): lax.all_to_all(tiles, axis, split_axis=0, concat_axis=0, tiled=True)  13.2 us
  transfers between devices with their start and end apart: 6, of which 5 were waited for; matrix products, arithmetic and copies ran while one was open for 4% of the time, Pallas kernels for 0%

commit v1 on v0

--- a/solution.py
+++ b/solution.py
@@ -9,6 +9,13 @@
 ROW = ("row_0", "row_1")
 ROW_COL = ("row_0", "row_1", "col_0", "col_1", "col_2")
 SHRINK = 0.9
+
+
+def exchange_gather(x, mesh_axis, d):
+    devices = lax.axis_size(mesh_axis)
+    tiles = jnp.stack([x for _ in range(devices)])
+    tiles = lax.all_to_all(tiles, mesh_axis, split_axis=0, concat_axis=0)
+    return jnp.concatenate(tiles, axis=d)
 
 
 def split_up(value, dim, peers):
@@ -35,7 +42,7 @@
 
 
 def apply_gram(gram_flat, operand):
-    panels = lax.all_gather(operand, COL, axis=1, tiled=True)
+    panels = exchange_gather(operand, COL, 1)
     partial_value = lax.slice_in_dim(gram_flat, 0, operand.shape[1] * lax.axis_size(ROW), axis=1)
     return sum_at_owner(
         jnp.einsum("ksi,kio->so", partial_value, panels, preferred_element_type=jnp.float32), ROW, 0

time: 422 us -> 510 us (1.21)
  blocking collectives: 83.9 us -> 249 us
  waiting for transfers between devices: 268 us -> 191 us
  local copies, waits for them, and re-layouts: 3.51 us -> 17.1 us
  between operations: 13.9 us -> 0.84 us
    all_gather x4 -> x0, waiting for transfers between devices: 260 us -> none  [apply_gram(): panels = lax.all_gather(operand, COL, axis=1, tiled=True)]
    all_to_all x0 -> x1, waiting for transfers between devices: none -> 183 us  [exchange_gather(): tiles = lax.all_to_all(tiles, mesh_axis, split_axis=0, concat_axis=0)]
    all_to_all x0 -> x3, blocking collectives: none -> 173 us  [exchange_gather(): tiles = lax.all_to_all(tiles, mesh_axis, split_axis=0, concat_axis=0)]
    reshape x0 -> x1, local copies, waits for them, and re-layouts: none -> 8.47 us  [exchange_gather(): return jnp.concatenate(tiles, axis=d)]
    all_to_all x2, blocking collectives: 43.3 us -> 36.9 us  [sum_at_owner(): lax.all_to_all(tiles, axis, split_axis=0, concat_axis=0, tiled=True)]
    all_to_all x0 -> x1, starting transfers between devices: none -> 5.29 us  [exchange_gather(): tiles = lax.all_to_all(tiles, mesh_axis, split_axis=0, concat_axis=0)]
  transfers between devices with their start and end apart: 6 -> 3, of which waited for: 5 -> 3; matrix products, arithmetic and copies ran while one was open for 4% -> 5% of each run, Pallas kernels for 0% -> 0%
where the time goes in v1:
time: 510 us; the launch traced here: 509 us
  blocking collectives  249 us (49%)
  waiting for transfers between devices  191 us (37%)
  other arithmetic  19.4 us (4%)
  starting transfers between devices  18 us (4%)
  local copies, waits for them, and re-layouts  17.1 us (3%)
  matrix products  13.8 us (3%)
    all_to_all x1, waiting for transfers between devices, exchange_gather(): tiles = lax.all_to_all(tiles, mesh_axis, split_axis=0, concat_axis=0)  183 us
    all_to_all x3, blocking collectives, exchange_gather(): tiles = lax.all_to_all(tiles, mesh_axis, split_axis=0, concat_axis=0)  173 us
    psum x5, blocking collectives, one_axis_at_a_time(): value = lax.psum(value, axis)  39.2 us
    all_to_all x2, blocking collectives, sum_at_owner(): lax.all_to_all(tiles, axis, split_axis=0, concat_axis=0, tiled=True)  36.9 us
    all_to_all x2, starting transfers between devices, sum_at_owner(): lax.all_to_all(tiles, axis, split_axis=0, concat_axis=0, tiled=True)  12.7 us
    dot_general x4, matrix products, apply_gram(): jnp.einsum('ksi,kio->so', partial_value, panels, preferred_element_type=j...  11.4 us
  transfers between devices with their start and end apart: 3, of which 3 were waited for; matrix products, arithmetic and copies ran while one was open for 5% of the time, Pallas kernels for 0%

profile of v1, /device:TPU:1, one launch (start us, length us, event | category | flops | bytes accessed | tf_op | source)
XLA Modules:
  0.0 508.7 jit_solution(4402069886753916995)
XLA Ops:
  0.7 1.5 copy-done
  2.3 0.3 copy.17
  2.7 0.7 gather_fusion
  3.5 1.1 convert_reduce_fusion.1
  4.6 0.3 stack.19
  4.9 61.7 %all_to_all.40 = bf16[32,1,32,1024]{3,2,1,0:T(8,128)(2,1)} all-to-all(bf16[32,1,32,1024]{3,2,1,0:T(8,128)(2,1)S(1)} %stack.19), channel_id=1, replica_groups=mesh['row_0'=4,'row_1'=2,'col_0'=8,'col_1'=2,'col_2'=2] {'col_0','col_1'..., dimensions={0} | all-to-all | bytes 4194304 | tf_op jit(solution)/shard_map/all_to_all | solution.py:17
  66.6 4.3 stack.18
  70.8 5.3 %all-to-all-start = ((bf16[32,4,32,1024]{3,2,1,0:T(8,128)(2,1)}), bf16[32,4,32,1024]{3,2,1,0:T(8,128)(2,1)}, u32[]{:S(2)}, u32[]{:S(2)}) async-start(bf16[32,4,32,1024]{3,2,1,0:T(8,128)(2,1)} %stack.18), calls=%async_computation | async-start | bytes 16777216 | tf_op jit(solution)/shard_map/all_to_all | solution.py:17
  76.1 0.4 reduce_sum.125
  76.6 3.3 fusion.20
  79.9 182.8 %all-to-all-done = bf16[32,4,32,1024]{3,2,1,0:T(8,128)(2,1)} async-done(((bf16[32,4,32,1024]{3,2,1,0:T(8,128)(2,1)}), bf16[32,4,32,1024]{3,2,1,0:T(8,128)(2,1)}, u32[]{:S(2)}, u32[]{:S(2)}) %all-to-all-start) | async-done | bytes 8388640 | tf_op jit(solution)/shard_map/all_to_all | solution.py:17
  262.7 6.4 %all-to-all-start.3 = ((f32[8,32,1024]{2,1,0:T(8,128)}), f32[8,32,1024]{2,1,0:T(8,128)}, u32[]{:S(2)}, u32[]{:S(2)}) async-start(f32[8,32,1024]{2,1,0:T(8,128)} %fusion.20), calls=%async_computation.3 | async-start | bytes 2097152 | tf_op jit(solution)/shard_map/all_to_all | solution.py:29
  269.4 8.5 %copy.14 = bf16[4,32,32,1024]{3,2,1,0:T(8,128)(2,1)} copy(bf16[4,32,32,1024]{3,2,0,1:T(8,128)(2,1)} %bitcast.10) | data formatting | bytes 16777216 | tf_op jit(solution)/shard_map/reshape | solution.py:18
  277.8 6.7 %fusion.2 = f32[8,32,1024]{2,1,0:T(8,128)} fusion(bf16[4,1024,1024,1]{2,1,3,0:T(8,128)(2,1)} %bitcast.87, bf16[4,8,1,32,1024]{4,3,2,1,0:T(8,128)(2,1)S(1)} %copy-done), kind=kOutput, calls=%fused_computation.3 | convolution fusion | flops 2147483648 | bytes 11534336 | tf_op jit(solution)/shard_map/ksi,kio->so/dot_general | solution.py:48
  284.6 0.3 all-to-all-done.3
  284.9 6.3 %all-to-all-start.1 = ((f32[8,32,1024]{2,1,0:T(8,128)}), f32[8,32,1024]{2,1,0:T(8,128)}, u32[]{:S(2)}, u32[]{:S(2)}) async-start(f32[8,32,1024]{2,1,0:T(8,128)} %fusion.2), calls=%async_computation.1 | async-start | bytes 2097152 | tf_op jit(solution)/shard_map/all_to_all | solution.py:29
  291.5 2.9 cholesky.19
  294.4 0.6 compare_reduce_fusion
  295.1 0.7 fusion.6
  295.8 2.4 custom-call.16
  298.2 1.3 reduce_sum.126
  299.5 7.5 %all-to-all-done.1 = f32[8,32,1024]{2,1,0:T(8,128)} async-done(((f32[8,32,1024]{2,1,0:T(8,128)}), f32[8,32,1024]{2,1,0:T(8,128)}, u32[]{:S(2)}, u32[]{:S(2)}) %all-to-all-start.1) | async-done | bytes 1048608 | tf_op jit(solution)/shard_map/all_to_all | solution.py:29
  307.0 1.3 reduce_sum.123
  308.3 0.7 multiply_reduce_fusion.3
  309.0 0.3 fusion.13
  309.3 0.3 fusion.18
  309.8 54.2 %all_to_all.41 = bf16[32,1,32,1024]{3,2,1,0:T(8,128)(2,1)S(1)} all-to-all(bf16[32,1,32,1024]{3,2,1,0:T(8,128)(2,1)S(1)} %stack.20), channel_id=1, replica_groups=mesh['row_0'=4,'row_1'=2,'col_0'=8,'col_1'=2,'col_2'=2] {'col_0','col_1'..., dimensions={0} | all-to-all | bytes 4194304 | tf_op jit(solution)/shard_map/all_to_all | solution.py:17
  364.1 0.7 fusion.21
  364.8 18.7 %all_to_all.42 = f32[8,32,1024]{2,1,0:T(8,128)} all-to-all(f32[8,32,1024]{2,1,0:T(8,128)S(1)} %fusion.21), channel_id=1, replica_groups=mesh['row_0'=4,'row_1'=2,'col_0'=8,'col_1'=2,'col_2'=2] {'row_0','row_1'}, dimensions={0} | all-to-all | bytes 2097152 | tf_op jit(solution)/shard_map/all_to_all | solution.py:29
  383.5 1.3 reduce_sum.127
  384.8 0.7 multiply_reduce_fusion.2
  385.5 0.3 fusion.10
  385.8 0.3 fusion.19
  386.1 0.3 stack.21
  386.3 57.0 %all_to_all.43 = bf16[32,1,32,1024]{3,2,1,0:T(8,128)(2,1)S(1)} all-to-all(bf16[32,1,32,1024]{3,2,1,0:T(8,128)(2,1)S(1)} %stack.21), channel_id=1, replica_groups=mesh['row_0'=4,'row_1'=2,'col_0'=8,'col_1'=2,'col_2'=2] {'col_0','col_1'..., dimensions={0} | all-to-all | bytes 4194304 | tf_op jit(solution)/shard_map/all_to_all | solution.py:17
  443.3 0.7 fusion.22
  444.1 18.2 %all_to_all.44 = f32[8,32,1024]{2,1,0:T(8,128)S(1)} all-to-all(f32[8,32,1024]{2,1,0:T(8,128)S(1)} %fusion.22), channel_id=1, replica_groups=mesh['row_0'=4,'row_1'=2,'col_0'=8,'col_1'=2,'col_2'=2] {'row_0','row_1'}, dimensions={0} | all-to-all | bytes 2097152 | tf_op jit(solution)/shard_map/all_to_all | solution.py:29
  462.3 1.5 multiply_reduce_fusion.1
  463.8 2.6 pad_maximum_fusion
  466.4 6.9 %psum.35 = f32[4]{0:T(128)S(1)} all-reduce(f32[4]{0:T(128)S(1)} %pad_maximum_fusion), channel_id=1, replica_groups=mesh['row_0'=4,'row_1'=2,'col_0'=8,'col_1'=2,'col_2'=2] {'row_0'}, use_global_device_ids=true, to_apply=%region_15.18 | all-reduce | flops 4 | bytes 32 | tf_op jit(solution)/shard_map/psum | solution.py:35
  473.4 5.3 %psum.36 = f32[4]{0:T(128)S(1)} all-reduce(f32[4]{0:T(128)S(1)} %psum.35), channel_id=1, replica_groups=mesh['row_0'=4,'row_1'=2,'col_0'=8,'col_1'=2,'col_2'=2] {'row_1'}, use_global_device_ids=true, to_apply=%region_16.19 | all-reduce | flops 4 | bytes 32 | tf_op jit(solution)/shard_map/psum | solution.py:35
  478.6 10.7 %psum.37 = f32[4]{0:T(128)S(1)} all-reduce(f32[4]{0:T(128)S(1)} %psum.36), channel_id=1, replica_groups=mesh['row_0'=4,'row_1'=2,'col_0'=8,'col_1'=2,'col_2'=2] {'col_0'}, use_global_device_ids=true, to_apply=%region_17.20 | all-reduce | flops 4 | bytes 32 | tf_op jit(solution)/shard_map/psum | solution.py:35
  489.3 0.3 fusion.7
  489.6 4.4 psum.38
  494.0 0.9 convolution_add_fusion
  494.9 11.9 %psum.39 = f32[4]{0:T(128)S(1)} all-reduce(f32[4]{0:T(128)S(1)} %psum.38), channel_id=1, replica_groups=mesh['row_0'=4,'row_1'=2,'col_0'=8,'col_1'=2,'col_2'=2] {'col_2'}, use_global_device_ids=true, to_apply=%region_19.22 | all-reduce | flops 4 | bytes 32 | tf_op jit(solution)/shard_map/psum | solution.py:35
  506.9 0.7 slice.17
  507.5 1.2 divide_sqrt_fusion
  (20 shorter events, 1.1 us)
Async XLA Ops:
  0.6 1.6 copy-start
  4.9 61.7 %copy-start.1 = (bf16[4,32,1024]{2,1,0:T(8,128)(2,1)S(1)}, bf16[4,32,1024]{2,1,0:T(8,128)(2,1)}, u32[]{:S(2)}) copy-start(bf16[4,32,1024]{2,1,0:T(8,128)(2,1)} %param.7) | copy-start | bytes 786436
  70.8 191.9 %all-to-all-start = ((bf16[32,4,32,1024]{3,2,1,0:T(8,128)(2,1)}), bf16[32,4,32,1024]{3,2,1,0:T(8,128)(2,1)}, u32[]{:S(2)}, u32[]{:S(2)}) async-start(bf16[32,4,32,1024]{3,2,1,0:T(8,128)(2,1)} %stack.18), calls=%async_computation | async-start | bytes 16777216 | tf_op jit(solution)/shard_map/all_to_all | solution.py:17
  262.7 22.2 %all-to-all-start.3 = ((f32[8,32,1024]{2,1,0:T(8,128)}), f32[8,32,1024]{2,1,0:T(8,128)}, u32[]{:S(2)}, u32[]{:S(2)}) async-start(f32[8,32,1024]{2,1,0:T(8,128)} %fusion.20), calls=%async_computation.3 | async-start | bytes 2097152 | tf_op jit(solution)/shard_map/all_to_all | solution.py:29
  284.9 22.1 %all-to-all-start.1 = ((f32[8,32,1024]{2,1,0:T(8,128)}), f32[8,32,1024]{2,1,0:T(8,128)}, u32[]{:S(2)}, u32[]{:S(2)}) async-start(f32[8,32,1024]{2,1,0:T(8,128)} %fusion.2), calls=%async_computation.1 | async-start | bytes 2097152 | tf_op jit(solution)/shard_map/all_to_all | solution.py:29
  298.2 86.6 %copy-start.2 = (f32[32]{0:T(128)}, f32[32]{0:T(128)S(1)}, u32[]{:S(2)}) copy-start(f32[32]{0:T(128)S(1)} %get-tuple-element.14) | copy-start | bytes 388
